TPU v7x, 256 devices: a whole 4x4x8 slice. The times are simulated.
256 devices in a mesh: tower: 16 (over z, x_hi), dev: 16 (over x_lo, y, core).
Axes of the slice: x: 4 (x_hi: 2, x_lo: 2; x = x_hi * 2 + x_lo), y: 4, z: 8, core: 2. Of those that a mesh axis runs over, the one named last changes fastest.
Arguments:
- ids: int32 [16, 16, 2048, 32], P('tower', 'dev'), may hold values from 0 to 511
- tables: bfloat16 [16, 16, 512, 128], P('tower', 'dev'), may hold values from -1 to 1
- order: int32 [2048], replicated, may hold values from 0 to 2047, each once
- w_first: bfloat16 [16, 2048, 1024], P('tower', 'dev'), may hold values from -0.125 to 0.125
- w_second: bfloat16 [16, 1024, 512], P('tower'), may hold values from -0.1875 to 0.1875
- w_head: bfloat16 [8192, 128], replicated, may hold values from -0.0625 to 0.0625
- w_interact: float32 [256, 128], replicated, may hold values from -0.1875 to 0.1875
Outputs:
- scores: float32 [16, 128, 128], P('dev', 'tower')
Inputs may be any that keep to these rules, and one draw needn't show every extreme that they name: order is a permutation of the batch rows 0 to 2047.
All inputs are finite; a program needn't handle non-finite values.
Results may differ from a plain program's by a relative error of at most 0.0023.
Values may be sent and summed in bfloat16 or wider, within the bound.
A program may use at most 64 MiB of HBM per device.

v0:
```python
import math
import jax
import jax.numpy as jnp
from jax import lax
from jax.sharding import PartitionSpec as P


def pool_feature(feature_ids, table):
    samples = feature_ids.shape[0]
    active = table.shape[0]
    block = math.gcd(samples, 512)
    blocked = feature_ids.reshape(samples // block, block, feature_ids.shape[1])
    positions = lax.broadcasted_iota(jnp.int32, (1, 1, active), 2)

    def pool_block(block_ids):
        tally = jnp.sum((block_ids[:, :, None] == positions).astype(jnp.int32), axis=1)
        return jnp.dot(
            tally.astype(jnp.bfloat16), table, preferred_element_type=jnp.float32
        ).astype(jnp.bfloat16)

    pooled = lax.map(pool_block, blocked)
    return pooled.reshape(samples, table.shape[1])


def on_device(ids, tables, order, w_first, w_second, w_head, w_interact):
    towers = lax.axis_size("tower")
    devices = lax.axis_size("dev")
    samples = ids.shape[2]
    my_rows = samples // devices
    pieces = pool_feature(ids[0, 0], tables[0, 0])
    features = jnp.take(pieces, order, axis=0)
    received = lax.all_to_all(features, "dev", split_axis=0, concat_axis=1, tiled=True)
    preact = jnp.dot(
        received,
        lax.all_gather(w_first[0], "dev", axis=0, tiled=True),
        preferred_element_type=jnp.float32,
    )
    hidden = jnp.maximum(preact, 0.0).astype(jnp.bfloat16)
    outputs = jnp.dot(hidden, w_second[0], preferred_element_type=jnp.float32).astype(jnp.bfloat16)
    width = outputs.shape[1]
    share = my_rows // towers
    gathered = lax.all_to_all(
        outputs.reshape(1, towers, share, width), "tower", split_axis=1, concat_axis=0, tiled=True
    )[:, 0]
    amount = gathered.shape[1]
    joined = jnp.transpose(gathered, (1, 0, 2)).reshape(amount, towers * width)
    head = jnp.dot(joined, w_head, preferred_element_type=jnp.float32)
    widened = gathered.astype(jnp.float32)
    products = jnp.einsum(
        "tmz,smz->mts", widened, widened, precision=lax.Precision.HIGHEST
    ) / math.sqrt(width)
    interact_term = jnp.dot(
        products.reshape(amount, towers * towers), w_interact, precision=lax.Precision.HIGHEST
    )
    scored = head + interact_term
    return scored[None]


def solution(mesh):
    return jax.shard_map(
        on_device,
        mesh=mesh,
        in_specs=(
            P("tower", "dev", None, None),
            P("tower", "dev", None, None),
            P(),
            P("tower", "dev", None),
            P("tower", None, None),
            P(),
            P(),
        ),
        out_specs=P("dev", "tower", None),
        check_vma=False,
    )
```

profile of v0, /device:TPU:1, one launch (start us, length us, event | category | flops | bytes accessed | tf_op | source)
XLA Modules:
  0.0 118.9 jit_solution(7275496688290093356)
XLA Ops:
  6.5 0.0 copy-start
  6.5 0.0 all-gather.3.cloned.1.call-start
  6.5 0.7 all-gather.3.cloned.1.call-update
  7.3 2.3 %copy.17 = s32[1,1,2048,32]{3,2,1,0:T(8,128)} copy(s32[1,1,2048,32]{2,3,1,0:T(8,128)} %param.9) | data formatting | bytes 524288 | tf_op args[0]
  9.5 0.7 fusion.27
  10.2 53.5 %while.11 = (s32[]{:T(128)}, bf16[4,512,128]{2,1,0:T(8,128)(2,1)S(1)}, s32[4,512,32]{2,1,0:T(8,128)}, bf16[512,128]{1,0:T(8,128)(2,1)}, s32[]{:T(128)}) while((s32[]{:T(128)}, bf16[4,512,128]{2,1,0:T(8,128)(2,1)S(1)}, s32[4,512,32]{2,1,0:T(8,128)}, bf16[512,128]{1,0:T(8,128)(2,1)}, s32[]{:T(128)}) %tuple.27), condition=%wide.region_2.3_spmd.clone, body=%wide.region_0.2_spmd.clone.sunk | while | flops 92340224 | bytes 2555973 | solution.py:21
  10.2 1.0 dynamic-slice_bitcast_fusion.2
  11.2 11.1 %convert_reduce_fusion.2 = s32[512,512]{1,0:T(8,128)S(1)} fusion(s32[512,32]{1,0:T(8,128)S(1)} %dynamic-slice_bitcast_fusion.2), kind=kLoop, calls=%fused_computation.3.clone.1 | loop fusion | flops 24903680 | bytes 1114112 | tf_op jit(solution)/shard_map/while/body/eval_jaxpr/reduce_sum | solution.py:16
  22.4 1.3 %fusion.41 = bf16[4,512,128]{2,1,0:T(8,128)(2,1)S(1)} fusion(bf16[4,512,128]{2,1,0:T(8,128)(2,1)S(1)} %get-tuple-element.82, s32[]{:T(128)} %get-tuple-element.81, bf16[512,128]{1,0:T(8,128)(2,1)} %get-tuple-element.89, s32[512,512]{1,0:T(8,128)S(1)} %convert_reduce_fusion.2), kind=kOutput, calls=%fused_computation.6.clone.1 | convolution fusion | flops 67436544 | bytes 1310724 | tf_op jit(solution)/shard_map/while/body/eval_jaxpr/dot_general | solution.py:17
  23.6 1.0 dynamic-slice_bitcast_fusion.2
  24.6 11.1 %convert_reduce_fusion.2 = s32[512,512]{1,0:T(8,128)S(1)} fusion(s32[512,32]{1,0:T(8,128)S(1)} %dynamic-slice_bitcast_fusion.2), kind=kLoop, calls=%fused_computation.3.clone.1 | loop fusion | flops 24903680 | bytes 1114112 | tf_op jit(solution)/shard_map/while/body/eval_jaxpr/reduce_sum | solution.py:16
  35.7 1.3 %fusion.41 = bf16[4,512,128]{2,1,0:T(8,128)(2,1)S(1)} fusion(bf16[4,512,128]{2,1,0:T(8,128)(2,1)S(1)} %get-tuple-element.82, s32[]{:T(128)} %get-tuple-element.81, bf16[512,128]{1,0:T(8,128)(2,1)} %get-tuple-element.89, s32[512,512]{1,0:T(8,128)S(1)} %convert_reduce_fusion.2), kind=kOutput, calls=%fused_computation.6.clone.1 | convolution fusion | flops 67436544 | bytes 1310724 | tf_op jit(solution)/shard_map/while/body/eval_jaxpr/dot_general | solution.py:17
  37.0 1.0 dynamic-slice_bitcast_fusion.2
  38.0 11.1 %convert_reduce_fusion.2 = s32[512,512]{1,0:T(8,128)S(1)} fusion(s32[512,32]{1,0:T(8,128)S(1)} %dynamic-slice_bitcast_fusion.2), kind=kLoop, calls=%fused_computation.3.clone.1 | loop fusion | flops 24903680 | bytes 1114112 | tf_op jit(solution)/shard_map/while/body/eval_jaxpr/reduce_sum | solution.py:16
  49.1 1.3 %fusion.41 = bf16[4,512,128]{2,1,0:T(8,128)(2,1)S(1)} fusion(bf16[4,512,128]{2,1,0:T(8,128)(2,1)S(1)} %get-tuple-element.82, s32[]{:T(128)} %get-tuple-element.81, bf16[512,128]{1,0:T(8,128)(2,1)} %get-tuple-element.89, s32[512,512]{1,0:T(8,128)S(1)} %convert_reduce_fusion.2), kind=kOutput, calls=%fused_computation.6.clone.1 | convolution fusion | flops 67436544 | bytes 1310724 | tf_op jit(solution)/shard_map/while/body/eval_jaxpr/dot_general | solution.py:17
  50.4 1.0 dynamic-slice_bitcast_fusion.2
  51.4 11.1 %convert_reduce_fusion.2 = s32[512,512]{1,0:T(8,128)S(1)} fusion(s32[512,32]{1,0:T(8,128)S(1)} %dynamic-slice_bitcast_fusion.2), kind=kLoop, calls=%fused_computation.3.clone.1 | loop fusion | flops 24903680 | bytes 1114112 | tf_op jit(solution)/shard_map/while/body/eval_jaxpr/reduce_sum | solution.py:16
  62.5 1.3 %fusion.41 = bf16[4,512,128]{2,1,0:T(8,128)(2,1)S(1)} fusion(bf16[4,512,128]{2,1,0:T(8,128)(2,1)S(1)} %get-tuple-element.82, s32[]{:T(128)} %get-tuple-element.81, bf16[512,128]{1,0:T(8,128)(2,1)} %get-tuple-element.89, s32[512,512]{1,0:T(8,128)S(1)} %convert_reduce_fusion.2), kind=kOutput, calls=%fused_computation.6.clone.1 | convolution fusion | flops 67436544 | bytes 1310724 | tf_op jit(solution)/shard_map/while/body/eval_jaxpr/dot_general | solution.py:17
  63.8 0.0 copy-start.2
  63.8 6.2 %gather_fusion = bf16[2048,128]{1,0:T(8,128)(2,1)S(1)} fusion(bf16[2048,128]{1,0:T(8,128)(2,1)S(1)} %bitcast.58, s32[2048]{0:T(1024)S(1)} %fusion.27), kind=kCustom, calls=%fused_computation | custom fusion | bytes 1056768 | tf_op jit(solution)/shard_map/jit(_take)/gather | solution.py:31
  70.0 0.3 copy.18
  70.3 0.0 copy-done.2
  70.3 0.1 broadcast_select_fusion
  70.4 16.4 %all_to_all.25 = bf16[16,128,128]{1,2,0:T(8,128)(2,1)S(1)} all-to-all(bf16[16,128,128]{1,2,0:T(8,128)(2,1)S(1)} %broadcast_select_fusion), channel_id=1, replica_groups=mesh['tower'=16,'dev'=16] {'dev'}, dimensions={0} | all-to-all | bytes 1048576 | tf_op jit(solution)/shard_map/all_to_all | solution.py:32
  86.8 3.5 %fusion.19 = bf16[1,16,8,512]{3,2,0,1:T(8,128)(2,1)S(1)} fusion(bf16[128,2048]{0,1:T(8,128)(2,1)S(1)} %bitcast.61, bf16[1,2048,1024]{2,1,0:T(8,128)(2,1)} %all-gather.3.cloned.1.call-done, bf16[1,1024,512]{2,1,0:T(8,128)(2,1)} %param.13), kind=kOutput, calls=%fused_computation.15 | convolution fusion | flops 671416320 | bytes 5898240 | tf_op jit(solution)/shard_map/dot_general | solution.py:39
  90.2 20.2 %all_to_all.26 = bf16[1,16,8,512]{3,2,0,1:T(8,128)(2,1)S(1)} all-to-all(bf16[1,16,8,512]{3,2,0,1:T(8,128)(2,1)S(1)} %fusion.19), channel_id=1, replica_groups=mesh['tower'=16,'dev'=16] {'tower'}, dimensions={1} | all-to-all | bytes 262144 | tf_op jit(solution)/shard_map/all_to_all | solution.py:42
  110.5 0.1 copy.21
  110.6 0.2 convolution_multiply_fusion
  110.8 0.1 reshape.35
  110.9 0.0 copy-done
  110.9 0.4 fusion.29
  111.3 0.8 fusion.22
  (6 shorter events, 0.1 us)
Async XLA Ops:
  6.5 104.3 %copy-start = (bf16[8192,128]{1,0:T(8,128)(2,1)S(1)}, bf16[8192,128]{1,0:T(8,128)(2,1)}, u32[]{:S(2)}) copy-start(bf16[8192,128]{1,0:T(8,128)(2,1)} %param.14) | copy-start | bytes 6291460
  6.5 80.2 %all-gather.3.cloned.1.call-start = ((), (), s32[]{:S(2)}) async-start(), calls=%async_computation.2 | async-start | bytes 4456448 | tf_op jit(solution)/shard_map/all_gather | solution.py:35
  63.8 6.5 %copy-start.2 = (s32[2048]{0:T(1024)S(1)}, s32[2048]{0:T(1024)}, u32[]{:S(2)}) copy-start(s32[2048]{0:T(1024)} %param.11) | copy-start | bytes 24580
  86.8 24.5 %copy-start.1 = (f32[256,128]{1,0:T(8,128)S(1)}, f32[256,128]{1,0:T(8,128)}, u32[]{:S(2)}) copy-start(f32[256,128]{1,0:T(8,128)} %param.15) | copy-start | bytes 393220
Sparse Core Ops, SparseCore 0:
  9.2 43.9 all-gather.2
where the time goes:
time: 119 us
  other arithmetic  45.3 us (38%)
  blocking collectives  36.6 us (31%)
  between operations  13.5 us (11%)
  local copies, waits for them, and re-layouts  12.9 us (11%)
  matrix products  9.84 us (8%)
    reduce_sum x4, other arithmetic, pool_block(): jnp.sum((block_ids[:, :, None] == positions).astype(jnp.int32), axis=1)  44.5 us
    all_to_all x1, blocking collectives, on_device(): lax.all_to_all(outputs.reshape(1, towers, share, width), 'tower', split_a...  20.2 us
    all_to_all x1, blocking collectives, on_device(): lax.all_to_all(features, 'dev', split_axis=0, concat_axis=1, tiled=True)  16.4 us
    gather x2, local copies, waits for them, and re-layouts, on_device(): features = jnp.take(pieces, order, axis=0)  6.46 us
    dot_general x4, matrix products, pool_block(): jnp.dot(tally.astype(jnp.bfloat16), table, preferred_element_type=jnp.flo...  5.05 us
    eq x4, local copies, waits for them, and re-layouts, pool_block(): block_ids[:, :, None] == positions  3.88 us
    dot_general x1, matrix products, on_device(): jnp.dot(hidden, w_second[0], preferred_element_type=jnp.float32)  3.47 us
  transfers between devices with their start and end apart: 1, of which 0 were waited for; matrix products, arithmetic and copies ran while one was open for 53% of the time, Pallas kernels for 0%

commit v1 on v0

--- a/solution.py
+++ b/solution.py
@@ -3,6 +3,13 @@
 import jax.numpy as jnp
 from jax import lax
 from jax.sharding import PartitionSpec as P
+
+
+def trade_parts(value, name, split, join):
+    size = lax.axis_size(name)
+    pieces = jnp.stack(jnp.split(value, size, axis=split), axis=0)
+    pieces = lax.all_to_all(pieces, name, split_axis=0, concat_axis=0)
+    return jnp.concatenate(pieces, axis=join)
 
 
 def pool_feature(feature_ids, table):
@@ -39,9 +46,7 @@
     outputs = jnp.dot(hidden, w_second[0], preferred_element_type=jnp.float32).astype(jnp.bfloat16)
     width = outputs.shape[1]
     share = my_rows // towers
-    gathered = lax.all_to_all(
-        outputs.reshape(1, towers, share, width), "tower", split_axis=1, concat_axis=0, tiled=True
-    )[:, 0]
+    gathered = trade_parts(outputs.reshape(1, towers, share, width), "tower", 1, 0)[:, 0]
     amount = gathered.shape[1]
     joined = jnp.transpose(gathered, (1, 0, 2)).reshape(amount, towers * width)
     head = jnp.dot(joined, w_head, preferred_element_type=jnp.float32)

time: 119 us -> 119 us (level)
    unnamed x8 -> x23, local copies, waits for them, and re-layouts: 2.37 us -> 2.41 us
where the time goes in v1:
time: 119 us
  other arithmetic  45.3 us (38%)
  blocking collectives  36.6 us (31%)
  between operations  13.6 us (11%)
  local copies, waits for them, and re-layouts  12.9 us (11%)
  matrix products  9.84 us (8%)
    reduce_sum x4, other arithmetic, pool_block(): jnp.sum((block_ids[:, :, None] == positions).astype(jnp.int32), axis=1)  44.5 us
    all_to_all x1, blocking collectives, trade_parts(): pieces = lax.all_to_all(pieces, name, split_axis=0, concat_axis=0)  20.2 us
    all_to_all x1, blocking collectives, on_device(): lax.all_to_all(features, 'dev', split_axis=0, concat_axis=1, tiled=True)  16.4 us
    gather x2, local copies, waits for them, and re-layouts, on_device(): features = jnp.take(pieces, order, axis=0)  6.46 us
    dot_general x4, matrix products, pool_block(): jnp.dot(tally.astype(jnp.bfloat16), table, preferred_element_type=jnp.flo...  5.05 us
    eq x4, local copies, waits for them, and re-layouts, pool_block(): block_ids[:, :, None] == positions  3.88 us
    dot_general x1, matrix products, on_device(): jnp.dot(hidden, w_second[0], preferred_element_type=jnp.float32)  3.47 us
    unnamed x23, local copies, waits for them, and re-layouts  2.41 us
  transfers between devices with their start and end apart: 1, of which 0 were waited for; matrix products, arithmetic and copies ran while one was open for 53% of the time, Pallas kernels for 0%

profile of v1, /device:TPU:1, one launch (start us, length us, event | category | flops | bytes accessed | tf_op | source)
XLA Modules:
  0.0 119.1 jit_solution(6995948571340571670)
XLA Ops:
  6.5 0.0 copy-start
  6.5 0.0 all-gather.3.cloned.1.call-start
  6.5 0.7 all-gather.3.cloned.1.call-update
  7.3 2.3 %copy.300 = s32[1,1,2048,32]{3,2,1,0:T(8,128)} copy(s32[1,1,2048,32]{2,3,1,0:T(8,128)} %param.9) | data formatting | bytes 524288 | tf_op args[0]
  9.5 0.7 fusion.27
  10.2 53.5 %while.11 = (s32[]{:T(128)}, bf16[4,512,128]{2,1,0:T(8,128)(2,1)S(1)}, s32[4,512,32]{2,1,0:T(8,128)}, bf16[512,128]{1,0:T(8,128)(2,1)}, s32[]{:T(128)}) while((s32[]{:T(128)}, bf16[4,512,128]{2,1,0:T(8,128)(2,1)S(1)}, s32[4,512,32]{2,1,0:T(8,128)}, bf16[512,128]{1,0:T(8,128)(2,1)}, s32[]{:T(128)}) %tuple.27), condition=%wide.region_2.3_spmd.clone, body=%wide.region_0.2_spmd.clone.sunk | while | flops 92340224 | bytes 2555973 | solution.py:28
  10.2 1.0 dynamic-slice_bitcast_fusion.2
  11.2 11.1 %convert_reduce_fusion.2 = s32[512,512]{1,0:T(8,128)S(1)} fusion(s32[512,32]{1,0:T(8,128)S(1)} %dynamic-slice_bitcast_fusion.2), kind=kLoop, calls=%fused_computation.3.clone.1 | loop fusion | flops 24903680 | bytes 1114112 | tf_op jit(solution)/shard_map/while/body/eval_jaxpr/reduce_sum | solution.py:23
  22.4 1.3 %fusion.41 = bf16[4,512,128]{2,1,0:T(8,128)(2,1)S(1)} fusion(bf16[4,512,128]{2,1,0:T(8,128)(2,1)S(1)} %get-tuple-element.82, s32[]{:T(128)} %get-tuple-element.81, bf16[512,128]{1,0:T(8,128)(2,1)} %get-tuple-element.89, s32[512,512]{1,0:T(8,128)S(1)} %convert_reduce_fusion.2), kind=kOutput, calls=%fused_computation.6.clone.1 | convolution fusion | flops 67436544 | bytes 1310724 | tf_op jit(solution)/shard_map/while/body/eval_jaxpr/dot_general | solution.py:24
  23.6 1.0 dynamic-slice_bitcast_fusion.2
  24.6 11.1 %convert_reduce_fusion.2 = s32[512,512]{1,0:T(8,128)S(1)} fusion(s32[512,32]{1,0:T(8,128)S(1)} %dynamic-slice_bitcast_fusion.2), kind=kLoop, calls=%fused_computation.3.clone.1 | loop fusion | flops 24903680 | bytes 1114112 | tf_op jit(solution)/shard_map/while/body/eval_jaxpr/reduce_sum | solution.py:23
  35.7 1.3 %fusion.41 = bf16[4,512,128]{2,1,0:T(8,128)(2,1)S(1)} fusion(bf16[4,512,128]{2,1,0:T(8,128)(2,1)S(1)} %get-tuple-element.82, s32[]{:T(128)} %get-tuple-element.81, bf16[512,128]{1,0:T(8,128)(2,1)} %get-tuple-element.89, s32[512,512]{1,0:T(8,128)S(1)} %convert_reduce_fusion.2), kind=kOutput, calls=%fused_computation.6.clone.1 | convolution fusion | flops 67436544 | bytes 1310724 | tf_op jit(solution)/shard_map/while/body/eval_jaxpr/dot_general | solution.py:24
  37.0 1.0 dynamic-slice_bitcast_fusion.2
  38.0 11.1 %convert_reduce_fusion.2 = s32[512,512]{1,0:T(8,128)S(1)} fusion(s32[512,32]{1,0:T(8,128)S(1)} %dynamic-slice_bitcast_fusion.2), kind=kLoop, calls=%fused_computation.3.clone.1 | loop fusion | flops 24903680 | bytes 1114112 | tf_op jit(solution)/shard_map/while/body/eval_jaxpr/reduce_sum | solution.py:23
  49.1 1.3 %fusion.41 = bf16[4,512,128]{2,1,0:T(8,128)(2,1)S(1)} fusion(bf16[4,512,128]{2,1,0:T(8,128)(2,1)S(1)} %get-tuple-element.82, s32[]{:T(128)} %get-tuple-element.81, bf16[512,128]{1,0:T(8,128)(2,1)} %get-tuple-element.89, s32[512,512]{1,0:T(8,128)S(1)} %convert_reduce_fusion.2), kind=kOutput, calls=%fused_computation.6.clone.1 | convolution fusion | flops 67436544 | bytes 1310724 | tf_op jit(solution)/shard_map/while/body/eval_jaxpr/dot_general | solution.py:24
  50.4 1.0 dynamic-slice_bitcast_fusion.2
  51.4 11.1 %convert_reduce_fusion.2 = s32[512,512]{1,0:T(8,128)S(1)} fusion(s32[512,32]{1,0:T(8,128)S(1)} %dynamic-slice_bitcast_fusion.2), kind=kLoop, calls=%fused_computation.3.clone.1 | loop fusion | flops 24903680 | bytes 1114112 | tf_op jit(solution)/shard_map/while/body/eval_jaxpr/reduce_sum | solution.py:23
  62.5 1.3 %fusion.41 = bf16[4,512,128]{2,1,0:T(8,128)(2,1)S(1)} fusion(bf16[4,512,128]{2,1,0:T(8,128)(2,1)S(1)} %get-tuple-element.82, s32[]{:T(128)} %get-tuple-element.81, bf16[512,128]{1,0:T(8,128)(2,1)} %get-tuple-element.89, s32[512,512]{1,0:T(8,128)S(1)} %convert_reduce_fusion.2), kind=kOutput, calls=%fused_computation.6.clone.1 | convolution fusion | flops 67436544 | bytes 1310724 | tf_op jit(solution)/shard_map/while/body/eval_jaxpr/dot_general | solution.py:24
  63.8 0.0 copy-start.2
  63.8 6.2 %gather_fusion = bf16[2048,128]{1,0:T(8,128)(2,1)S(1)} fusion(bf16[2048,128]{1,0:T(8,128)(2,1)S(1)} %bitcast.120, s32[2048]{0:T(1024)S(1)} %fusion.27), kind=kCustom, calls=%fused_computation | custom fusion | bytes 1056768 | tf_op jit(solution)/shard_map/jit(_take)/gather | solution.py:38
  70.0 0.3 copy.301
  70.3 0.0 copy-done.2
  70.3 0.1 broadcast_select_fusion
  70.4 16.4 %all_to_all.21 = bf16[16,128,128]{1,2,0:T(8,128)(2,1)S(1)} all-to-all(bf16[16,128,128]{1,2,0:T(8,128)(2,1)S(1)} %broadcast_select_fusion), channel_id=1, replica_groups=mesh['tower'=16,'dev'=16] {'dev'}, dimensions={0} | all-to-all | bytes 1048576 | tf_op jit(solution)/shard_map/all_to_all | solution.py:39
  86.8 3.5 %fusion.19 = bf16[1,16,8,512]{3,2,1,0:T(8,128)(2,1)S(1)} fusion(bf16[128,2048]{0,1:T(8,128)(2,1)S(1)} %bitcast.123, bf16[1,2048,1024]{2,1,0:T(8,128)(2,1)} %all-gather.3.cloned.1.call-done, bf16[1,1024,512]{2,1,0:T(8,128)(2,1)} %param.13), kind=kOutput, calls=%fused_computation.15 | convolution fusion | flops 671416320 | bytes 5898240 | tf_op jit(solution)/shard_map/dot_general | solution.py:46
  90.4 20.2 %all_to_all.22 = bf16[16,1,1,8,512]{4,3,2,1,0:T(8,128)(2,1)S(1)} all-to-all(bf16[16,1,1,8,512]{4,3,2,1,0:T(8,128)(2,1)S(1)} %constant_dynamic-update-slice_fusion), channel_id=1, replica_groups=mesh['tower'=16,'dev'=16] {'tower'}, dimensions={0} | all-to-all | bytes 262144 | tf_op jit(solution)/shard_map/all_to_all | solution.py:11
  110.7 0.1 copy.303
  110.8 0.2 convolution_multiply_fusion
  111.0 0.1 reshape.31
  111.1 0.0 copy-done
  111.1 0.4 fusion.29
  111.5 0.8 fusion.22
  (22 shorter events, 0.1 us)
Async XLA Ops:
  6.5 104.5 %copy-start = (bf16[8192,128]{1,0:T(8,128)(2,1)S(1)}, bf16[8192,128]{1,0:T(8,128)(2,1)}, u32[]{:S(2)}) copy-start(bf16[8192,128]{1,0:T(8,128)(2,1)} %param.14) | copy-start | bytes 6291460
  6.5 80.2 %all-gather.3.cloned.1.call-start = ((), (), s32[]{:S(2)}) async-start(), calls=%async_computation.2 | async-start | bytes 4456448 | tf_op jit(solution)/shard_map/all_gather | solution.py:42
  63.8 6.5 %copy-start.2 = (s32[2048]{0:T(1024)S(1)}, s32[2048]{0:T(1024)}, u32[]{:S(2)}) copy-start(s32[2048]{0:T(1024)} %param.11) | copy-start | bytes 24580
  86.8 24.7 %copy-start.1 = (f32[256,128]{1,0:T(8,128)S(1)}, f32[256,128]{1,0:T(8,128)}, u32[]{:S(2)}) copy-start(f32[256,128]{1,0:T(8,128)} %param.15) | copy-start | bytes 393220
Sparse Core Ops, SparseCore 0:
  9.2 43.9 all-gather.2
